TPU v7x, 32 devices: a whole 2x2x4 slice. The times are simulated.
32 devices in a mesh: tm: 8 (over z, y), row: 2 (over core), col: 2 (over x).
Axes of the slice: x: 2, y: 2, z: 4, core: 2. Of those that a mesh axis runs over, the one named last changes fastest.
Arguments:
- precision_diag: float32 [16, 512, 512], P('tm', 'row', 'col'), may hold values from -4 to 16
- precision_link: float32 [16, 512, 512], P('tm', 'row', 'col'), may hold values from -8 to 2
Outputs:
- pivots: float32 [16, 512, 512], P('tm', 'row', 'col')
- couplings: float32 [16, 512, 512], P('tm', 'row', 'col')
- log_variance: float32 [16, 512], P('tm', ('row', 'col'))
All inputs are finite; a program needn't handle non-finite values.
Results may differ from a plain program's by a relative error of at most 0.0003.
Values sent between devices are 32-bit elements; how exact they have to be, the bound alone decides.
A program may use at most 128 MiB of HBM per device.

v0:
```python
import jax
import jax.numpy as jnp
from jax import lax
from jax.experimental import pallas as pl
from jax.experimental.pallas import tpu as pltpu
from jax.sharding import PartitionSpec as P

LEVELS = 4

LANES = 128
ROWS = 8
GROUP = 32


def hdot(left, right, dims=((1,), (0,))):
    return lax.dot_general(
        left, right, (dims, ((), ())), precision=lax.Precision.HIGHEST, preferred_element_type=jnp.float32
    )


def split_three(array):
    high = array.astype(jnp.bfloat16)
    rest = array - high.astype(jnp.float32)
    middle = rest.astype(jnp.bfloat16)
    return high, middle, (rest - middle.astype(jnp.float32)).astype(jnp.bfloat16)


def packed_dot(left, right):
    high, middle, low = split_three(left)
    first, second, third = split_three(right)
    wide = jnp.concatenate([high, high, middle, middle, high, low], axis=1)
    tall = jnp.concatenate([first, second, first, second, third, first], axis=0)
    return jnp.dot(wide, tall, preferred_element_type=jnp.float32)


def sweep_group(strips, start):
    sub = lax.broadcasted_iota(jnp.int32, (ROWS, LANES), 0)
    lane = lax.broadcasted_iota(jnp.int32, (ROWS, LANES), 1)
    pick = lambda strip, row: jnp.broadcast_to(strip[row : row + 1, :], (ROWS, LANES))
    strips = list(strips)
    count = len(strips)

    def spread(strip, p):
        return [
            jnp.broadcast_to(strip[:, start + ROWS * p + j : start + ROWS * p + j + 1], (ROWS, LANES)) for j in range(ROWS)
        ]

    def total(terms):
        while len(terms) > 1:
            terms = [terms[m] + terms[m + 1] for m in range(0, len(terms), 2)]
        return terms[0]

    cols = spread(strips[0], 0)
    for p in range(count):
        base = start + ROWS * p
        inside = (lane >= base) & (lane < base + ROWS)
        panel = jnp.where(inside, jnp.where(lane - base == sub, 1.0, 0.0), strips[p])
        if p + 1 < count:
            ahead_cols = spread(strips[p], p + 1)
            next_left = spread(strips[p + 1], p)
            next_cols = spread(strips[p + 1], p + 1)
        for i in range(0, ROWS, 2):
            first, second = cols[i], cols[i + 1]
            on_first, on_second = sub == i, sub == i + 1
            outside = (sub < i) | (sub > i + 1)
            a, b = pick(first, i), pick(first, i + 1)
            d = pick(second, i + 1)
            det = a * d - b * b
            scale = pl.reciprocal(det, approx=True)
            left = jnp.where(on_first, d, jnp.where(on_second, -b, second * b - first * d))
            right = jnp.where(on_second, a, jnp.where(on_first, -b, first * b - second * a))
            scale = scale * (2.0 - det * scale)
            apply = lambda strip: jnp.where(outside, strip, 0.0) + scale * (left * pick(strip, i) + right * pick(strip, i + 1))
            panel = apply(panel)
            for j in range(i + 2, ROWS):
                cols[j] = apply(cols[j])
            if p + 1 < count:
                ahead_cols = [apply(strip) for strip in ahead_cols]
        if p + 1 < count:
            cols = [
                next_cols[j] - total([next_left[m] * pick(ahead_cols[j], m) for m in range(ROWS)])
                for j in range(ROWS)
            ]
        for q in [q for q in range(p + 1, count)] + [q for q in range(p)]:
            left_cols = next_left if q == p + 1 else spread(strips[q], p)
            strips[q] = jnp.where(inside, 0.0, strips[q]) - total(
                [c * pick(panel, j) for j, c in enumerate(left_cols)]
            )
        strips[p] = panel
    return strips


def invert_lanes(block):
    lane = lax.broadcasted_iota(jnp.int32, (LANES, LANES), 1)
    for start in range(0, LANES, GROUP):
        strips = [block[start + ROWS * q : start + ROWS * (q + 1), :] for q in range(GROUP // ROWS)]
        solved = sweep_group(strips, start)
        inside = (lane >= start) & (lane < start + GROUP)
        above = [jnp.zeros((start, LANES), jnp.float32)] if start else []
        rest = LANES - start - GROUP
        below = [jnp.zeros((rest, LANES), jnp.float32)] if rest else []
        padded = jnp.concatenate(above + solved + below, axis=0)
        update = packed_dot(jnp.where(inside, block, 0.0), padded)
        block = jnp.where(inside, 0.0, block) - update
        block = jnp.concatenate(
            ([block[:start, :]] if start else []) + solved + ([block[start + GROUP :, :]] if rest else []), axis=0
        )
    return block


def invert_ref(work, between, first_block=0):
    node_count = work.shape[0]

    def step(k, carry):
        between(k)
        block_id = lax.rem(k + first_block, node_count // LANES)
        here = pl.ds(pl.multiple_of(block_id * LANES, LANES), LANES)
        inverse = invert_lanes(work[here, here])
        solved = packed_dot(inverse, work[here, :])
        column = work[:, here]
        work[:, here] = jnp.zeros((node_count, LANES), jnp.float32)
        row_block = lax.broadcasted_iota(jnp.int32, (node_count, LANES), 0) // LANES
        column = jnp.where(row_block == block_id, 0.0, column)
        col_block = lax.broadcasted_iota(jnp.int32, (LANES, node_count), 1) // LANES
        wide = jnp.concatenate([inverse] * (node_count // LANES), axis=1)
        solved = jnp.where(col_block == block_id, wide, solved)
        work[...] = work[...] - packed_dot(column, solved)
        work[here, :] = solved
        return carry

    lax.fori_loop(0, node_count // LANES, step, 0)


def cyclic_kernel(
    diag_ref, link_ref, pivot_ref, coupling_ref, log_ref,
    whole, work, made, ahead, back,
    x_send, x_recv, r_send, r_recv, f_send, f_recv,
    up_send, down_send, ahead_recv, back_recv,
):
    time_id, row_id, col_id = lax.axis_index("tm"), lax.axis_index("row"), lax.axis_index("col")
    times = lax.axis_size("tm")
    half = diag_ref.shape[1]
    node_count = 2 * half
    blocks = node_count // LANES
    reach = LEVELS - 1
    depth = sum((lax.rem(time_id, 2**j) == 0).astype(jnp.int32) for j in range(1, reach + 1))
    stride = sum(jnp.where(depth == j, 2**j, 0) for j in range(reach))
    mesh_id = pl.DeviceIdType.MESH

    def part(index):
        return pl.ds(pl.multiple_of(index * half, LANES), half)

    mine_rows, mine_cols = part(row_id), part(col_id)
    other_rows, other_cols = part(1 - row_id), part(1 - col_id)

    barrier = pltpu.get_barrier_semaphore()
    pl.semaphore_signal(barrier, inc=1, device_id={"col": 1 - col_id}, device_id_type=mesh_id)
    pl.semaphore_signal(barrier, inc=1, device_id={"row": 1 - row_id}, device_id_type=mesh_id)
    greeted = 2
    for j in range(reach):
        for by in (-(2**j), 2**j):
            near = (depth >= j) & (time_id + by >= 0) & (time_id + by < times)

            @pl.when(near)
            def _(by=by):
                pl.semaphore_signal(barrier, inc=1, device_id={"tm": time_id + by}, device_id_type=mesh_id)

            greeted = greeted + near.astype(jnp.int32)
    pl.semaphore_wait(barrier, greeted)

    def copy(src, dst, send, recv, target):
        return pltpu.make_async_remote_copy(
            src_ref=src, dst_ref=dst, send_sem=send, recv_sem=recv, device_id=target, device_id_type=mesh_id
        )

    def phase(ph, carry):
        first = ph == 0
        later = ph == 1
        solving = first | (depth < reach)
        on_diag = row_id == col_id

        def x_copy(a):
            tile = whole.at[ph, a, mine_rows, mine_cols]
            return copy(tile, tile, x_send.at[ph, a], x_recv.at[ph, a], {"col": 1 - col_id})

        def r_copy(a):
            tile = whole.at[ph, a, mine_rows, mine_cols]
            return copy(tile, tile, r_send.at[ph, a], r_recv.at[ph, a], {"row": 1 - row_id})

        def f_copy(a):
            tile = whole.at[ph, a, mine_rows, other_cols]
            return copy(tile, tile, f_send.at[ph, a], f_recv.at[ph, a], {"row": 1 - row_id})

        def up_copy(kind, source, level, by):
            return copy(
                made.at[ph, source], ahead.at[level, kind], up_send.at[ph, kind], ahead_recv.at[level, kind],
                {"tm": time_id + by},
            )

        def down_copy(kind, source, level, by):
            return copy(
                made.at[ph, source], back.at[level, kind], down_send.at[kind], back_recv.at[level, kind],
                {"tm": time_id - by},
            )

        def received(kind, level):
            by = 1 if level == 0 else 2 ** (level - 1)

            def from_below(use):
                @pl.when((depth >= level) & (time_id >= by))
                def _():
                    up_copy(kind, 0, level, 0).wait_recv()
                    use(ahead)

            def from_above(use):
                if level > 0:

                    @pl.when(depth >= level)
                    def _():
                        down_copy(kind, 0, level, 0).wait_recv()
                        use(back)

            return from_below, from_above

        @pl.when(first)
        def _():
            whole[0, 0, mine_rows, mine_cols] = diag_ref[1]
            pivot_ref[1] = diag_ref[1]
            high = jnp.where(time_id == times - 1, 0.0, link_ref[1])
            coupling_ref[1] = high
            whole[0, 1, mine_rows, mine_cols] = link_ref[0]
            whole[0, 2, mine_rows, mine_cols] = high

        @pl.when(later)
        def _():
            pivot_ref[0] = diag_ref[0] - made[0, 1]
            for level in range(LEVELS):
                def subtract(source, level=level):
                    pivot_ref[0] = pivot_ref[0] - source[level, 0]

                for arrival in received(0, level):
                    arrival(subtract)
            whole[1, 0, mine_rows, mine_cols] = pivot_ref[0]

        @pl.when(on_diag)
        def _():
            x_copy(0).start()

        r_copy(0).start()
        r_copy(0).wait_recv()

        work[:, mine_cols] = whole[ph, 0, :, mine_cols]
        far = part(1 - col_id)
        work[far, other_cols] = jnp.zeros((half, half), jnp.float32)
        work[part(col_id), other_cols] = whole[ph, 0, far, mine_cols].T

        def between(k):
            @pl.when((k == 1) & jnp.logical_not(on_diag))
            def _():
                x_copy(0).wait_recv()
                f_copy(0).start()

            @pl.when(k == blocks // 2)
            def _():
                @pl.when(on_diag)
                def _():
                    f_copy(0).wait_recv()

                work[far, other_cols] = work[far, other_cols] + whole[ph, 0, far, other_cols]

            @pl.when(k == jnp.where(first, 0, 1))
            def _():
                @pl.when(later)
                def _():
                    coupling_ref[0] = made[0, 2]
                    for level in range(LEVELS):
                        def place_below(source, level=level):
                            whole[1, 1, mine_rows, mine_cols] = source[level, 1]

                        def place_above(source, level=level):
                            coupling_ref[0] = source[level, 1]

                        from_below, from_above = received(1, level)
                        from_below(place_below)
                        from_above(place_above)
                    whole[1, 2, mine_rows, mine_cols] = coupling_ref[0]

                @pl.when(solving)
                def _():
                    for a in (2, 1):
                        x_copy(a).start()
                        r_copy(a).start()

            @pl.when((k == blocks - 1) & solving)
            def _():
                x_copy(2).wait_recv()
                f_copy(2).start()

        invert_ref(work, between, col_id * (blocks // 2))

        spot = pl.ds(pl.multiple_of((2 * row_id + col_id) * (node_count // 4), LANES), node_count // 4)
        corner = work[spot, spot]
        same = lax.broadcasted_iota(jnp.int32, corner.shape, 0) == lax.broadcasted_iota(jnp.int32, corner.shape, 1)
        log_ref[pl.ds(1 - ph, 1), :] = jnp.log(jnp.sum(jnp.where(same, corner, 0.0), axis=0, keepdims=True))

        @pl.when(solving)
        def _():
            x_copy(1).wait_recv()
            f_copy(1).start()
            r_copy(2).wait_recv()
            f_copy(2).wait_recv()
            above_row = whole[ph, 2, mine_rows, :]
            level = jnp.where(first, 0, depth + 1)
            by = jnp.where(first, 1, stride)
            goes_up = time_id + by < times
            reached = hdot(work[...], whole[ph, 2, part(col_id), :], ((1,), (1,)))
            made[ph, 0] = hdot(above_row, reached)

            @pl.when(goes_up)
            def _():
                up_copy(0, 0, level, by).start()

            r_copy(1).wait_recv()
            solved = hdot(work[...], whole[ph, 1, :, mine_cols])
            f_copy(1).wait_recv()
            made[ph, 1] = hdot(whole[ph, 1, :, part(row_id)], solved, ((0,), (0,)))

            @pl.when(later)
            def _():
                down_copy(0, 1, level, by).start()

            made[ph, 2] = -hdot(above_row, solved)

            @pl.when(goes_up)
            def _():
                up_copy(1, 2, level, by).start()

            @pl.when(later)
            def _():
                down_copy(1, 2, level, by).start()

            for a in (1, 2):
                x_copy(a).wait_send()
                r_copy(a).wait_send()
                f_copy(a).wait_send()

        r_copy(0).wait_send()

        @pl.when(on_diag)
        def _():
            x_copy(0).wait_send()

        @pl.when(jnp.logical_not(on_diag))
        def _():
            f_copy(0).wait_send()

        @pl.when(later)
        def _():
            @pl.when(time_id + 1 < times)
            def _():
                for kind in (0, 1):
                    copy(
                        made.at[0, 2 * kind], ahead.at[0, kind], up_send.at[0, kind], ahead_recv.at[0, kind],
                        {"tm": time_id + 1},
                    ).wait_send()

            @pl.when(depth < reach)
            def _():
                for kind in (0, 1):
                    down_copy(kind, 1 + kind, depth + 1, stride).wait_send()

                    @pl.when(time_id + stride < times)
                    def _(kind=kind):
                        up_copy(kind, 2 * kind, depth + 1, stride).wait_send()

        return carry

    lax.fori_loop(0, 2, phase, 0)


def shards(precision_diag, precision_link):
    half = precision_diag.shape[1]
    node_count = 2 * half
    vmem = pl.BlockSpec(memory_space=pltpu.VMEM)
    dma = pltpu.SemaphoreType.DMA
    tile = (half, half)
    stack = jax.ShapeDtypeStruct(precision_diag.shape, jnp.float32)
    return pl.pallas_call(
        cyclic_kernel,
        out_shape=(stack, stack, jax.ShapeDtypeStruct((2, node_count // 4), jnp.float32)),
        in_specs=[vmem, vmem],
        out_specs=(vmem, vmem, vmem),
        scratch_shapes=[
            pltpu.VMEM((2, 3, node_count, node_count), jnp.float32),
            pltpu.VMEM((node_count, node_count), jnp.float32),
            pltpu.VMEM((2, 3) + tile, jnp.float32),
            pltpu.VMEM((LEVELS, 2) + tile, jnp.float32),
            pltpu.VMEM((LEVELS, 2) + tile, jnp.float32),
            dma((2, 3)), dma((2, 3)), dma((2, 3)), dma((2, 3)), dma((2, 3)), dma((2, 3)),
            dma((2, 2)), dma((2,)), dma((LEVELS, 2)), dma((LEVELS, 2)),
        ],
        compiler_params=pltpu.CompilerParams(collective_id=0, has_side_effects=True),
    )(precision_diag, precision_link)


def solution(mesh):
    in_specs = (P("tm", "row", "col"), P("tm", "row", "col"))
    out_specs = (P("tm", "row", "col"), P("tm", "row", "col"), P("tm", ("row", "col")))
    return jax.shard_map(shards, mesh=mesh, in_specs=in_specs, out_specs=out_specs, check_vma=False)
```

profile of v0, /device:TPU:0, one launch (start us, length us, event | category | flops | bytes accessed | tf_op | source)
XLA Modules:
  0.0 165.7 jit_solution(12614360791967803198)
XLA Ops:
  0.6 161.8 %shard_map.49 = (f32[2,256,256]{2,1,0:T(8,128)}, f32[2,256,256]{2,1,0:T(8,128)}, f32[2,128]{1,0:T(2,128)}) custom-call(f32[2,256,256]{2,1,0:T(8,128)} %diag_ref.1, f32[2,256,256]{2,1,0:T(8,128)} %link_ref.1), custom_call_target="tpu_custom_call" | custom-call | tf_op jit(solution)/shard_map/pallas_call | solution.py:388
  162.4 0.0 copy-start
  162.5 1.9 %copy.8 = f32[2,256,256]{2,1,0:T(8,128)} copy(f32[2,256,256]{2,1,0:T(8,128)} %get-tuple-element.6) | data formatting | bytes 1048576
  164.4 0.0 copy-done
  164.4 0.0 copy-start.1
  164.4 0.8 copy.9
  165.2 0.0 copy-done.1
  165.2 0.6 copy.10
Async XLA Ops:
  162.4 1.9 %copy-start = (f32[2,256,256]{2,1,0:T(8,128)S(1)}, f32[2,256,256]{2,1,0:T(8,128)}, u32[]{:S(2)}) copy-start(f32[2,256,256]{2,1,0:T(8,128)} %get-tuple-element.7) | copy-start | bytes 1572868
  164.4 0.8 copy-start.1
where the time goes:
time: 167 us; the launch traced here: 166 us
  Pallas kernels  162 us (97%)
  local copies, waits for them, and re-layouts  3.29 us (2%)
    pallas_call x1, Pallas kernels, shards(): pl.pallas_call(cyclic_kernel, out_shape=(stack, stack, jax.ShapeDtypeStru...  162 us

commit v1 on v0

v1 whole, which is shorter than its diff:
```python
import jax
import jax.numpy as jnp
from jax import lax
from jax.experimental import pallas as pl
from jax.experimental.pallas import tpu as pltpu
from jax.sharding import PartitionSpec as P

LEVELS = 4

LANES = 128
ROWS = 8
GROUP = 32


def split_three(array):
    high = array.astype(jnp.bfloat16)
    rest = array - high.astype(jnp.float32)
    middle = rest.astype(jnp.bfloat16)
    return high, middle, (rest - middle.astype(jnp.float32)).astype(jnp.bfloat16)


def packed_dot(left, right):
    high, middle, low = split_three(left)
    first, second, third = split_three(right)
    wide = jnp.concatenate([high, high, middle, middle, high, low], axis=1)
    tall = jnp.concatenate([first, second, first, second, third, first], axis=0)
    return jnp.dot(wide, tall, preferred_element_type=jnp.float32)


def sweep_group(strips, start):
    sub = lax.broadcasted_iota(jnp.int32, (ROWS, LANES), 0)
    lane = lax.broadcasted_iota(jnp.int32, (ROWS, LANES), 1)
    pick = lambda strip, row: jnp.broadcast_to(strip[row : row + 1, :], (ROWS, LANES))
    strips = list(strips)
    count = len(strips)

    def spread(strip, p):
        return [
            jnp.broadcast_to(strip[:, start + ROWS * p + j : start + ROWS * p + j + 1], (ROWS, LANES)) for j in range(ROWS)
        ]

    def total(terms):
        while len(terms) > 1:
            terms = [terms[m] + terms[m + 1] for m in range(0, len(terms), 2)]
        return terms[0]

    cols = spread(strips[0], 0)
    for p in range(count):
        base = start + ROWS * p
        inside = (lane >= base) & (lane < base + ROWS)
        panel = jnp.where(inside, jnp.where(lane - base == sub, 1.0, 0.0), strips[p])
        if p + 1 < count:
            ahead_cols = spread(strips[p], p + 1)
            next_left = spread(strips[p + 1], p)
            next_cols = spread(strips[p + 1], p + 1)
        for i in range(0, ROWS, 2):
            first, second = cols[i], cols[i + 1]
            on_first, on_second = sub == i, sub == i + 1
            outside = (sub < i) | (sub > i + 1)
            a, b = pick(first, i), pick(first, i + 1)
            d = pick(second, i + 1)
            det = a * d - b * b
            scale = pl.reciprocal(det, approx=True)
            left = jnp.where(on_first, d, jnp.where(on_second, -b, second * b - first * d))
            right = jnp.where(on_second, a, jnp.where(on_first, -b, first * b - second * a))
            scale = scale * (2.0 - det * scale)
            apply = lambda strip: jnp.where(outside, strip, 0.0) + scale * (left * pick(strip, i) + right * pick(strip, i + 1))
            panel = apply(panel)
            for j in range(i + 2, ROWS):
                cols[j] = apply(cols[j])
            if p + 1 < count:
                ahead_cols = [apply(strip) for strip in ahead_cols]
        if p + 1 < count:
            cols = [
                next_cols[j] - total([next_left[m] * pick(ahead_cols[j], m) for m in range(ROWS)])
                for j in range(ROWS)
            ]
        for q in [q for q in range(p + 1, count)] + [q for q in range(p)]:
            left_cols = next_left if q == p + 1 else spread(strips[q], p)
            strips[q] = jnp.where(inside, 0.0, strips[q]) - total(
                [c * pick(panel, j) for j, c in enumerate(left_cols)]
            )
        strips[p] = panel
    return strips


def split_two(array):
    high = array.astype(jnp.bfloat16)
    return high, (array - high.astype(jnp.float32)).astype(jnp.bfloat16)


def wide_left(array):
    high, low = split_two(array)
    return jnp.concatenate([high, high, low], axis=1)


def wide_right(array):
    high, low = split_two(array)
    return jnp.concatenate([high, low, high], axis=1)


def tall_right(array):
    high, low = split_two(array)
    return jnp.concatenate([high, low, high], axis=0)


def mul(wide, tall):
    return jnp.dot(wide, tall, preferred_element_type=jnp.float32)


def mul_nt(wide, other):
    return lax.dot_general(wide, other, (((1,), (1,)), ((), ())), preferred_element_type=jnp.float32)


def invert_lanes(block, middle):
    lane = lax.broadcasted_iota(jnp.int32, (LANES, LANES), 1)
    for start in range(0, LANES, GROUP):
        if start == LANES // 2:
            middle()
        strips = [block[start + ROWS * q : start + ROWS * (q + 1), :] for q in range(GROUP // ROWS)]
        solved = sweep_group(strips, start)
        inside = (lane >= start) & (lane < start + GROUP)
        above = [jnp.zeros((start, LANES), jnp.float32)] if start else []
        rest = LANES - start - GROUP
        below = [jnp.zeros((rest, LANES), jnp.float32)] if rest else []
        padded = jnp.concatenate(above + solved + below, axis=0)
        update = packed_dot(jnp.where(inside, block, 0.0), padded)
        block = jnp.where(inside, 0.0, block) - update
        block = jnp.concatenate(
            ([block[:start, :]] if start else []) + solved + ([block[start + GROUP :, :]] if rest else []), axis=0
        )
    return block


def sweep_ref(work, before, middle, after):
    node_count = work.shape[0]

    def step(k, carry):
        before(k)
        here = pl.ds(pl.multiple_of(k * LANES, LANES), LANES)
        inverse = invert_lanes(work[here, here], lambda: middle(k))
        after(k)
        row_block = lax.broadcasted_iota(jnp.int32, (node_count, LANES), 0) // LANES
        column = jnp.where(row_block == k, 0.0, work[:, here])
        wide = wide_right(column)
        solved = mul(wide_left(column), tall_right(inverse))
        across = mul_nt(wide_left(inverse), wide)
        work[...] = work[...] - mul_nt(wide_left(solved), wide)
        work[:, here] = solved
        work[here, :] = across
        work[here, here] = -inverse
        return carry

    lax.fori_loop(0, node_count // LANES, step, 0)


def cyclic_kernel(
    diag_ref, link_ref, pivot_ref, coupling_ref, log_ref,
    base, links, work, solved, packed, landed, final, link_out, base_out, home_tiles, log_out, home_log,
    dx_send, dx_recv, dr_send, dr_recv, df_send, df_recv,
    lx_send, lx_recv, lr_send, lr_recv, lf_send, lf_recv,
    up_send, up_recv, pass_send, pass_recv, link_send, link_recv, base_send, base_recv, home_send, home_recv,
):
    time_id, row_id, col_id = lax.axis_index("tm"), lax.axis_index("row"), lax.axis_index("col")
    times = lax.axis_size("tm")
    half = diag_ref.shape[1]
    chunk = half // 2
    node_count = 2 * half
    blocks = node_count // LANES
    reach = LEVELS - 1
    mesh_id = pl.DeviceIdType.MESH
    power = lambda p: sum(jnp.where(p == j, 2**j, 0) for j in range(LEVELS))
    depth = sum((lax.rem(time_id + 1, 2**j) == 0).astype(jnp.int32) for j in range(1, LEVELS))
    keeps_all = depth == reach
    phases = depth + 1 + keeps_all.astype(jnp.int32)
    mine = jnp.where(row_id == col_id, 0, 1)
    leads = mine == 0
    low, high = pl.ds(0, half), pl.ds(half, half)
    part = lambda index: pl.ds(pl.multiple_of(index * half, LANES), half)
    ours = part(mine)
    starts = [sum(node_count - LANES * i for i in range(j)) for j in range(blocks + 1)]
    strip = (node_count - LANES) // 2
    rest = (starts[blocks] - starts[2]) // 2

    def copy(src, dst, send, recv, target):
        return pltpu.make_async_remote_copy(
            src_ref=src, dst_ref=dst, send_sem=send, recv_sem=recv, device_id=target, device_id_type=mesh_id
        )

    sibling, across_x = {"row": 1 - row_id}, {"col": 1 - col_id}

    level_of = 1 + sum((lax.rem(time_id, 2**j) == 0).astype(jnp.int32) for j in range(1, LEVELS))
    is_home = level_of > 1
    home_from = time_id + power(level_of - 1) - 1
    edges = [(time_id + power(depth), time_id + power(depth) < times)]
    for p in range(LEVELS):
        below = (p < depth) | (keeps_all & (p == reach))
        edges.append((time_id - 2**p, below & (time_id >= 2**p)))
    for p in range(2, LEVELS + 1):
        edges.append((time_id + 1 - 2 ** (p - 1), p < phases))
    edges.append((home_from, is_home))

    barrier = pltpu.get_barrier_semaphore()
    pl.semaphore_signal(barrier, inc=1, device_id=sibling, device_id_type=mesh_id)
    pl.semaphore_signal(barrier, inc=1, device_id=across_x, device_id_type=mesh_id)
    greeted = 2
    for other, near in edges:
        @pl.when(near)
        def _(other=other):
            pl.semaphore_signal(barrier, inc=1, device_id={"tm": other}, device_id_type=mesh_id)

        greeted = greeted + near.astype(jnp.int32)
    pl.semaphore_wait(barrier, greeted)

    def dx_copy(ph):
        return copy(base.at[ph, ours, low], base.at[ph, part(1 - mine), high], dx_send.at[ph], dx_recv.at[ph], across_x)

    def dx_arrival(ph):
        tile = base.at[ph, ours, high]
        return copy(tile, tile, dx_send.at[ph], dx_recv.at[ph], across_x)

    def dr_copy(ph):
        tile = base.at[ph, ours, low]
        return copy(tile, tile, dr_send.at[ph], dr_recv.at[ph], sibling)

    def df_copy(ph):
        tile = base.at[ph, high, high]
        return copy(tile, tile, df_send.at[ph], df_recv.at[ph], sibling)

    def start_base(ph):
        dr_copy(ph).start()

        @pl.when(leads)
        def _():
            dx_copy(ph).start()

    def link_tile(ph, slot, j, where):
        turned = (ph == 0) if slot == 0 else False
        own = jnp.where(turned, 0, mine * half) + j * chunk, jnp.where(turned, mine * half, 0)
        away = jnp.where(turned, half, (1 - mine) * half) + j * chunk, jnp.where(turned, (1 - mine) * half, half)
        got = jnp.where(turned, half, mine * half) + j * chunk, jnp.where(turned, mine * half, half)
        row, col = {"own": own, "away": away, "got": got}[where]
        return links.at[ph, slot, pl.ds(pl.multiple_of(row, LANES), chunk), pl.ds(pl.multiple_of(col, LANES), half)]

    def lx_copy(ph, slot, j):
        sems = lx_send.at[ph, slot, j], lx_recv.at[ph, slot, j]
        return copy(link_tile(ph, slot, j, "own"), link_tile(ph, slot, j, "away"), *sems, across_x)

    def lx_arrival(ph, slot, j):
        tile = link_tile(ph, slot, j, "got")
        return copy(tile, tile, lx_send.at[ph, slot, j], lx_recv.at[ph, slot, j], across_x)

    def lr_copy(ph, slot, j):
        tile = link_tile(ph, slot, j, "own")
        return copy(tile, tile, lr_send.at[ph, slot, j], lr_recv.at[ph, slot, j], sibling)

    def lf_copy(ph, slot, j):
        tile = link_tile(ph, slot, j, "got")
        return copy(tile, tile, lf_send.at[ph, slot, j], lf_recv.at[ph, slot, j], sibling)

    def start_link(ph, slot, j):
        lx_copy(ph, slot, j).start()
        lr_copy(ph, slot, j).start()

    def pass_link(ph, slot, j):
        lx_arrival(ph, slot, j).wait_recv()
        lf_copy(ph, slot, j).start()

    def end_link(ph, slot, j):
        lr_copy(ph, slot, j).wait_recv()
        lf_copy(ph, slot, j).wait_recv()

    def piece(i):
        if i == 0:
            return pl.ds(0, LANES)
        first, size = ((LANES, strip), (starts[1], strip), (starts[2], rest))[i - 1]
        if i == 2:
            size = (starts[2] - starts[1]) // 2
        return pl.ds(pl.multiple_of(first + row_id * size, 8), size)

    def up_copy(p, i):
        return copy(packed.at[1, piece(i)], landed.at[p, piece(i)], up_send.at[i], up_recv.at[p, i], {"tm": time_id + power(p)})

    def pass_copy(p, i):
        tile = landed.at[p, piece(i)]
        return copy(tile, tile, pass_send.at[p, i], pass_recv.at[p, i], sibling)

    def link_copy(p, j):
        rows = pl.ds(pl.multiple_of(mine * half + j * chunk, LANES), chunk)
        return copy(
            link_out.at[pl.ds(j * chunk, chunk)], links.at[p + 1, 0, rows, low], link_send.at[j], link_recv.at[p, j],
            {"tm": time_id + power(p)},
        )

    def base_copy(p):
        return copy(base_out, base.at[p + 2, ours, low], base_send.at[0], base_recv.at[p], {"tm": time_id + power(p)})

    def home_copy(ph, i):
        src = (final.at[ph - 1, ours], links.at[ph, 1, ours, low], log_out.at[ph])[i]
        dst = (home_tiles.at[0], home_tiles.at[1], home_log)[i]
        return copy(src, dst, home_send.at[ph, i], home_recv.at[i], {"tm": time_id + 1 - power(ph - 1)})

    def phase(ph, carry):
        first = ph == 0
        later = ph > 0
        solving = ph < LEVELS
        keeper = solving & ((ph < depth) | keeps_all)
        sender = (ph == depth) & jnp.logical_not(keeps_all)
        below = jnp.maximum(ph - 1, 0)
        joined = later & (time_id >= power(below))

        @pl.when(first)
        def _():
            base[0, ours, low] = diag_ref[1]
            start_base(0)
            upper = jnp.where(time_id == times - 1, 0.0, link_ref[1])
            links[0, 1, ours, low] = upper
            for j in (0, 1):
                start_link(0, 1, j)
            links[0, 0, low, ours] = link_ref[0].T
            for j in (0, 1):
                start_link(0, 0, j)
            base[1, ours, low] = diag_ref[0]

            @pl.when(depth > 0)
            def _():
                start_base(1)

            pivot_ref[1] = diag_ref[1]
            coupling_ref[1] = upper
            packed[0] = jnp.zeros(packed.shape[1:], jnp.float32)

        work[...] = jnp.zeros(work.shape, jnp.float32)
        dr_copy(ph).wait_recv()

        @pl.when(joined)
        def _():
            up_copy(below, 0).wait_recv()

        def absorb(j, top, bottom):
            cols = slice(LANES * j, LANES * (j + 1))
            rows = slice(top, bottom)
            lines = slice(starts[j] + top - LANES * j, starts[j] + bottom - LANES * j)
            value = base[ph, rows, cols] + packed[0, lines]
            work[rows, cols] = work[rows, cols] + value
            shown = LANES * j < half
            if shown:
                @pl.when(later)
                def _():
                    final[below, rows, cols] = value

            @pl.when(joined)
            def _():
                extra = landed[below, lines]
                work[rows, cols] = work[rows, cols] + extra
                if shown:
                    final[below, rows, cols] = value + extra

        def before(k):
            for j in range(blocks):
                @pl.when(k == j)
                def _(j=j):
                    if j in (1, 2):
                        @pl.when(joined)
                        def _():
                            pass_copy(below, j + 1).wait_recv()
                    if j == blocks // 2:
                        @pl.when(leads)
                        def _():
                            df_copy(ph).wait_recv()
                    if j == blocks - 1:
                        @pl.when(later & solving)
                        def _():
                            link_copy(below, 1).wait_recv()
                            start_link(ph, 0, 1)
                    absorb(j, LANES * j, node_count if j else LANES)

        def middle(k):
            @pl.when((k == 0) & joined)
            def _():
                up_copy(below, 1).wait_recv()
                pass_copy(below, 1).start()

            @pl.when(k == 1)
            def _():
                @pl.when(joined)
                def _():
                    up_copy(below, 3).wait_recv()
                    pass_copy(below, 3).start()

                @pl.when(jnp.logical_not(leads))
                def _():
                    dx_arrival(ph).wait_recv()
                    df_copy(ph).start()

            @pl.when(k == 2)
            def _():
                @pl.when(first)
                def _():
                    for j in (0, 1):
                        pass_link(0, 1, j)

                @pl.when(later & solving)
                def _():
                    link_copy(below, 0).wait_recv()
                    start_link(ph, 0, 0)

                @pl.when(later)
                def _():
                    @pl.when(leads)
                    def _():
                        for i in range(half // LANES):
                            for j in range(i + 1, half // LANES):
                                upper, lower = slice(LANES * i, LANES * (i + 1)), slice(LANES * j, LANES * (j + 1))
                                final[below, upper, lower] = final[below, lower, upper].T

                    @pl.when(ph == 1)
                    def _():
                        pivot_ref[0] = final[0, ours]
                        coupling_ref[0] = links[1, 1, ours, low]

                    @pl.when(ph > 1)
                    def _():
                        home_copy(ph, 0).start()
                        home_copy(ph, 1).start()

            @pl.when((k == 3) & solving)
            def _():
                pass_link(ph, 0, 0)

        def after(k):
            @pl.when(k == 0)
            def _():
                @pl.when(joined)
                def _():
                    pass_copy(below, 1).wait_recv()

                absorb(0, LANES, node_count)

                @pl.when(joined)
                def _():
                    up_copy(below, 2).wait_recv()
                    pass_copy(below, 2).start()

        sweep_ref(work, before, middle, after)

        spot = pl.ds(pl.multiple_of(mine * half + col_id * (node_count // 4), LANES), node_count // 4)
        corner = work[spot, spot]
        same = lax.broadcasted_iota(jnp.int32, corner.shape, 0) == lax.broadcasted_iota(jnp.int32, corner.shape, 1)
        logs = jnp.log(-jnp.sum(jnp.where(same, corner, 0.0), axis=0, keepdims=True))

        @pl.when(ph < 2)
        def _():
            log_ref[pl.ds(1 - ph, 1), :] = logs

        @pl.when(ph > 1)
        def _():
            log_out[ph] = jnp.broadcast_to(logs, log_out.shape[1:])
            home_copy(ph, 2).start()

        @pl.when(solving)
        def _():
            pass_link(ph, 0, 1)

            @pl.when(first)
            def _():
                for j in (0, 1):
                    end_link(0, 1, j)

            for j in (0, 1):
                end_link(ph, 0, j)
            near, far = jnp.where(keeper, 0, 1), jnp.where(keeper, 1, 0)
            inverse = tall_right(work[...])
            left = wide_left(links[ph, near])
            solved[...] = mul(left, inverse)

            def panel(j):
                return mul_nt(left[LANES * j :, :], wide_right(solved[LANES * j : LANES * (j + 1), :]))

            def add_up(j, value):
                lines = slice(starts[j], starts[j + 1])

                @pl.when(first)
                def _():
                    packed[1, lines] = value

                @pl.when(later)
                def _():
                    packed[1, lines] = packed[1, lines] + value

            @pl.when(keeper)
            def _():
                for j in range(blocks):
                    packed[0, starts[j] : starts[j + 1]] = panel(j)

                @pl.when(later)
                def _():
                    base_copy(below).wait_recv()
                    start_base(ph + 1)

                other = wide_left(links[ph, 1])
                links[ph + 1, 1] = mul_nt(other, wide_right(solved[...]))

                @pl.when(time_id + 1 < times)
                def _():
                    solved[...] = mul(other, inverse)
                    for j in range(blocks):
                        value = mul_nt(other[LANES * j :, :], wide_right(solved[LANES * j : LANES * (j + 1), :]))
                        add_up(j, value)

                @pl.when((ph == reach) & (time_id + power(reach) < times))
                def _():
                    for i in range(4):
                        up_copy(reach, i).start()

            @pl.when(sender)
            def _():
                for j in range(blocks):
                    add_up(j, panel(j))
                    if j == 0:
                        up_copy(ph, 0).start()
                        up_copy(ph, 1).start()
                    if j == 1:
                        up_copy(ph, 2).start()
                up_copy(ph, 3).start()
                other = wide_left(links[ph, 0, ours])
                link_out[...] = mul_nt(other, wide_right(solved[0:half, :]))
                for j in (0, 1):
                    link_copy(ph, j).start()

                @pl.when(later)
                def _():
                    base_copy(below).wait_recv()

                reached = mul(wide_left(links[ph, 0, low]), inverse)
                base_out[...] = base[ph + 1, ours, low] + mul_nt(other, wide_right(reached))
                base_copy(ph).start()

        return carry

    lax.fori_loop(0, phases, phase, 0)

    @pl.when(is_home)
    def _():
        for i in range(3):
            home_copy(2, i).wait_recv()
        pivot_ref[0] = home_tiles[0]
        coupling_ref[0] = home_tiles[1]
        log_ref[0:1, :] = home_log[0:1, :]

    def drain(ph, carry):
        below = jnp.maximum(ph - 1, 0)
        dr = (ph > 0) | (ph == 0)
        dr_copy(ph).wait_send()

        @pl.when(leads)
        def _():
            dx_copy(ph).wait_send()

        @pl.when(jnp.logical_not(leads))
        def _():
            df_copy(ph).wait_send()

        def link_sends(slot):
            for j in (0, 1):
                lx_copy(ph, slot, j).wait_send()
                lr_copy(ph, slot, j).wait_send()
                lf_copy(ph, slot, j).wait_send()

        @pl.when(ph < LEVELS)
        def _():
            link_sends(0)

        @pl.when(ph == 0)
        def _():
            link_sends(1)

        @pl.when((ph > 0) & (time_id >= power(below)))
        def _():
            for i in (1, 2, 3):
                pass_copy(below, i).wait_send()

        @pl.when(ph > 1)
        def _():
            for i in range(3):
                home_copy(ph, i).wait_send()

        return carry

    lax.fori_loop(0, phases, drain, 0)

    @pl.when(time_id + power(depth) < times)
    def _():
        for i in range(4):
            up_copy(depth, i).wait_send()

    @pl.when(depth < reach)
    def _():
        for j in (0, 1):
            link_copy(depth, j).wait_send()
        base_copy(depth).wait_send()


def shards(precision_diag, precision_link):
    half = precision_diag.shape[1]
    node_count = 2 * half
    blocks = node_count // LANES
    lines = LANES * LANES // LANES * blocks * (blocks + 1) // 2
    vmem = pl.BlockSpec(memory_space=pltpu.VMEM)
    dma = pltpu.SemaphoreType.DMA
    real = lambda *shape: pltpu.VMEM(shape, jnp.float32)
    stack = jax.ShapeDtypeStruct(precision_diag.shape, jnp.float32)
    phases = LEVELS + 1
    pair = (LEVELS, 2, 2)
    return pl.pallas_call(
        cyclic_kernel,
        out_shape=(stack, stack, jax.ShapeDtypeStruct((2, node_count // 4), jnp.float32)),
        in_specs=[vmem, vmem],
        out_specs=(vmem, vmem, vmem),
        scratch_shapes=[
            real(phases, node_count, node_count),
            real(phases, 2, node_count, node_count),
            real(node_count, node_count),
            real(node_count, node_count),
            real(2, lines, LANES),
            real(LEVELS, lines, LANES),
            real(LEVELS, node_count, half),
            real(half, half),
            real(half, half),
            real(2, half, half),
            real(phases, ROWS, node_count // 4),
            real(ROWS, node_count // 4),
            dma((phases,)), dma((phases,)), dma((phases,)), dma((phases,)), dma((phases,)), dma((phases,)),
            dma(pair), dma(pair), dma(pair), dma(pair), dma(pair), dma(pair),
            dma((4,)), dma((LEVELS, 4)), dma((LEVELS, 4)), dma((LEVELS, 4)),
            dma((2,)), dma((LEVELS, 2)), dma((1,)), dma((LEVELS,)), dma((phases, 3)), dma((3,)),
        ],
        compiler_params=pltpu.CompilerParams(collective_id=0, has_side_effects=True),
    )(precision_diag, precision_link)


def solution(mesh):
    in_specs = (P("tm", "row", "col"), P("tm", "row", "col"))
    out_specs = (P("tm", "row", "col"), P("tm", "row", "col"), P("tm", ("row", "col")))
    return jax.shard_map(shards, mesh=mesh, in_specs=in_specs, out_specs=out_specs, check_vma=False)
```

time: 167 us -> 141 us (0.84)
  Pallas kernels: 162 us -> 137 us
    pallas_call x1, Pallas kernels: 162 us -> 137 us  [shards(): pl.pallas_call(cyclic_kernel, out_shape=(stack, stack, jax.ShapeDtypeStru...]
where the time goes in v1:
time: 141 us
  Pallas kernels  137 us (97%)
  local copies, waits for them, and re-layouts  3.29 us (2%)
    pallas_call x1, Pallas kernels, shards(): pl.pallas_call(cyclic_kernel, out_shape=(stack, stack, jax.ShapeDtypeStru...  137 us
    unnamed x7, local copies, waits for them, and re-layouts  3.29 us

profile of v1, /device:TPU:0, one launch (start us, length us, event | category | flops | bytes accessed | tf_op | source)
XLA Modules:
  0.0 140.8 jit_solution(10444039903387719903)
XLA Ops:
  0.6 136.8 %shard_map.49 = (f32[2,256,256]{2,1,0:T(8,128)}, f32[2,256,256]{2,1,0:T(8,128)}, f32[2,128]{1,0:T(2,128)}) custom-call(f32[2,256,256]{2,1,0:T(8,128)} %diag_ref.1, f32[2,256,256]{2,1,0:T(8,128)} %link_ref.1), custom_call_target="tpu_custom_call" | custom-call | tf_op jit(solution)/shard_map/pallas_call | solution.py:615
  137.5 0.0 copy-start
  137.5 1.9 %copy.8 = f32[2,256,256]{2,1,0:T(8,128)} copy(f32[2,256,256]{2,1,0:T(8,128)} %get-tuple-element.6) | data formatting | bytes 1048576
  139.4 0.0 copy-done
  139.4 0.0 copy-start.1
  139.4 0.8 copy.9
  140.2 0.0 copy-done.1
  140.2 0.6 copy.10
Async XLA Ops:
  137.5 1.9 %copy-start = (f32[2,256,256]{2,1,0:T(8,128)S(1)}, f32[2,256,256]{2,1,0:T(8,128)}, u32[]{:S(2)}) copy-start(f32[2,256,256]{2,1,0:T(8,128)} %get-tuple-element.7) | copy-start | bytes 1572868
  139.4 0.8 copy-start.1

commit v2 on v1

--- a/solution.py
+++ b/solution.py
@@ -10,21 +10,7 @@
 LANES = 128
 ROWS = 8
 GROUP = 32
-
-
-def split_three(array):
-    high = array.astype(jnp.bfloat16)
-    rest = array - high.astype(jnp.float32)
-    middle = rest.astype(jnp.bfloat16)
-    return high, middle, (rest - middle.astype(jnp.float32)).astype(jnp.bfloat16)
-
-
-def packed_dot(left, right):
-    high, middle, low = split_three(left)
-    first, second, third = split_three(right)
-    wide = jnp.concatenate([high, high, middle, middle, high, low], axis=1)
-    tall = jnp.concatenate([first, second, first, second, third, first], axis=0)
-    return jnp.dot(wide, tall, preferred_element_type=jnp.float32)
+NEAR = 4
 
 
 def sweep_group(strips, start):
@@ -33,26 +19,27 @@
     pick = lambda strip, row: jnp.broadcast_to(strip[row : row + 1, :], (ROWS, LANES))
     strips = list(strips)
     count = len(strips)
-
-    def spread(strip, p):
-        return [
-            jnp.broadcast_to(strip[:, start + ROWS * p + j : start + ROWS * p + j + 1], (ROWS, LANES)) for j in range(ROWS)
-        ]
+    zero = strips[0] * 0.0
+
+    def spread(strip, p, columns):
+        base = start + ROWS * p
+        return [jnp.broadcast_to(strip[:, base + j : base + j + 1], (ROWS, LANES)) + zero for j in columns]
 
     def total(terms):
         while len(terms) > 1:
             terms = [terms[m] + terms[m + 1] for m in range(0, len(terms), 2)]
         return terms[0]
 
-    cols = spread(strips[0], 0)
+    near, far = range(NEAR), range(NEAR, ROWS)
+    cols = spread(strips[0], 0, range(ROWS))
     for p in range(count):
         base = start + ROWS * p
         inside = (lane >= base) & (lane < base + ROWS)
         panel = jnp.where(inside, jnp.where(lane - base == sub, 1.0, 0.0), strips[p])
         if p + 1 < count:
-            ahead_cols = spread(strips[p], p + 1)
-            next_left = spread(strips[p + 1], p)
-            next_cols = spread(strips[p + 1], p + 1)
+            ahead = spread(strips[p], p + 1, near)
+            next_left = spread(strips[p + 1], p, range(ROWS))
+            next_near = spread(strips[p + 1], p + 1, near)
         for i in range(0, ROWS, 2):
             first, second = cols[i], cols[i + 1]
             on_first, on_second = sub == i, sub == i + 1
@@ -64,22 +51,28 @@
             left = jnp.where(on_first, d, jnp.where(on_second, -b, second * b - first * d))
             right = jnp.where(on_second, a, jnp.where(on_first, -b, first * b - second * a))
             scale = scale * (2.0 - det * scale)
-            apply = lambda strip: jnp.where(outside, strip, 0.0) + scale * (left * pick(strip, i) + right * pick(strip, i + 1))
-            panel = apply(panel)
+            left_scaled, right_scaled = scale * left, scale * right
+
+            def soon(strip):
+                return jnp.where(outside, strip, 0.0) + scale * (left * pick(strip, i) + right * pick(strip, i + 1))
+
+            def apply(strip):
+                return jnp.where(outside, strip, 0.0) + (left_scaled * pick(strip, i) + right_scaled * pick(strip, i + 1))
+
             for j in range(i + 2, ROWS):
-                cols[j] = apply(cols[j])
+                cols[j] = (soon if j < i + 4 else apply)(cols[j])
+            last = i + 2 == ROWS
+            panel = (soon if last else apply)(panel)
             if p + 1 < count:
-                ahead_cols = [apply(strip) for strip in ahead_cols]
+                ahead = [(soon if last else apply)(strip) for strip in ahead]
         if p + 1 < count:
-            cols = [
-                next_cols[j] - total([next_left[m] * pick(ahead_cols[j], m) for m in range(ROWS)])
-                for j in range(ROWS)
-            ]
+            cols = [next_near[j] - total([next_left[m] * pick(ahead[j], m) for m in range(ROWS)]) for j in near]
+        rows = [pick(panel, j) for j in range(ROWS)]
         for q in [q for q in range(p + 1, count)] + [q for q in range(p)]:
-            left_cols = next_left if q == p + 1 else spread(strips[q], p)
-            strips[q] = jnp.where(inside, 0.0, strips[q]) - total(
-                [c * pick(panel, j) for j, c in enumerate(left_cols)]
-            )
+            left_cols = next_left if q == p + 1 else spread(strips[q], p, range(ROWS))
+            strips[q] = jnp.where(inside, 0.0, strips[q]) - total([c * rows[j] for j, c in enumerate(left_cols)])
+            if q == p + 1:
+                cols = cols + spread(strips[q], q, far)
         strips[p] = panel
     return strips
 
@@ -112,51 +105,82 @@
     return lax.dot_general(wide, other, (((1,), (1,)), ((), ())), preferred_element_type=jnp.float32)
 
 
-def invert_lanes(block, middle):
+def invert_lanes(block, middle=None, pause=LANES // 2):
     lane = lax.broadcasted_iota(jnp.int32, (LANES, LANES), 1)
-    for start in range(0, LANES, GROUP):
-        if start == LANES // 2:
+    groups = LANES // GROUP
+    for g in range(groups):
+        start = GROUP * g
+        if middle is not None and start == pause:
             middle()
+        inside = (lane >= start) & (lane < start + GROUP)
+        held = jnp.where(inside, block, 0.0)
+        high = held.astype(jnp.bfloat16).astype(jnp.float32)
+        low = held - high
+        both = (high + pltpu.roll(low, GROUP, axis=1)).astype(jnp.bfloat16)
+        twice = (both.astype(jnp.float32) + pltpu.roll(both.astype(jnp.float32), LANES // 2, axis=1)).astype(jnp.bfloat16)
+        kept = jnp.where(inside, 0.0, block)
         strips = [block[start + ROWS * q : start + ROWS * (q + 1), :] for q in range(GROUP // ROWS)]
         solved = sweep_group(strips, start)
-        inside = (lane >= start) & (lane < start + GROUP)
-        above = [jnp.zeros((start, LANES), jnp.float32)] if start else []
-        rest = LANES - start - GROUP
-        below = [jnp.zeros((rest, LANES), jnp.float32)] if rest else []
-        padded = jnp.concatenate(above + solved + below, axis=0)
-        update = packed_dot(jnp.where(inside, block, 0.0), padded)
-        block = jnp.where(inside, 0.0, block) - update
-        block = jnp.concatenate(
-            ([block[:start, :]] if start else []) + solved + ([block[start + GROUP :, :]] if rest else []), axis=0
-        )
+        first, second = split_two(jnp.concatenate(solved, axis=0))
+        pieces = [None] * groups
+        for at, value in enumerate((first, first, second, second)):
+            pieces[(g + at) % groups] = value
+        tall = jnp.concatenate(pieces, axis=0)
+        bands = {g: jnp.concatenate(solved, axis=0)}
+        order = [q for q in range(g + 1, groups)] + [q for q in range(g)]
+        for q in order:
+            rows = slice(GROUP * q, GROUP * (q + 1))
+            bands[q] = kept[rows] - mul(twice[rows], tall)
+        block = jnp.concatenate([bands[q] for q in range(groups)], axis=0)
     return block
 
 
-def sweep_ref(work, before, middle, after):
+def sweep_ref(work, pivot_ready, panel_ready, middle, prepare, early):
     node_count = work.shape[0]
-
-    def step(k, carry):
-        before(k)
-        here = pl.ds(pl.multiple_of(k * LANES, LANES), LANES)
-        inverse = invert_lanes(work[here, here], lambda: middle(k))
-        after(k)
-        row_block = lax.broadcasted_iota(jnp.int32, (node_count, LANES), 0) // LANES
-        column = jnp.where(row_block == k, 0.0, work[:, here])
+    blocks = node_count // LANES
+    span = lambda k: slice(LANES * k, LANES * (k + 1))
+    late = LANES - GROUP
+    pivot_ready(0)
+    inverse = invert_lanes(work[span(0), span(0)], lambda: middle(0), late)
+    for k in range(blocks):
+        here = span(k)
+        panel_ready(k)
+        if k == blocks - 1:
+            early(inverse)
+        column = work[:, here]
         wide = wide_right(column)
         solved = mul(wide_left(column), tall_right(inverse))
+        left = wide_left(solved)
+        if k + 1 < blocks:
+            pivot_ready(k + 1)
+            ahead = span(k + 1)
+            pivot = work[ahead, ahead] - mul_nt(left[ahead], wide[ahead])
         across = mul_nt(wide_left(inverse), wide)
-        work[...] = work[...] - mul_nt(wide_left(solved), wide)
-        work[:, here] = solved
-        work[here, :] = across
+        for j in range(blocks):
+            if j == k:
+                continue
+            cols = span(j)
+            pieces = [slice(0, LANES * k)] if k else []
+            if j > k:
+                top = LANES * (j + 1 if j == k + 1 else j)
+                pieces += [slice(top, node_count)] if top < node_count else []
+            for rows in pieces:
+                work[rows, cols] = work[rows, cols] - mul_nt(left[rows], wide[cols])
+            work[here, cols] = across[:, cols]
+        if k:
+            work[: LANES * k, here] = solved[: LANES * k]
         work[here, here] = -inverse
-        return carry
-
-    lax.fori_loop(0, node_count // LANES, step, 0)
+        if k + 2 < blocks:
+            inverse = invert_lanes(pivot, lambda: middle(k + 1), late if k == 0 else LANES // 2)
+        elif k + 1 < blocks:
+            prepare()
+            inverse = invert_lanes(pivot)
 
 
 def cyclic_kernel(
     diag_ref, link_ref, pivot_ref, coupling_ref, log_ref,
     base, links, work, solved, packed, landed, final, link_out, base_out, home_tiles, log_out, home_log,
+    part_sum, part_solved, last_panel, last_across, last_solved,
     dx_send, dx_recv, dr_send, dr_recv, df_send, df_recv,
     lx_send, lx_recv, lr_send, lr_recv, lf_send, lf_recv,
     up_send, up_recv, pass_send, pass_recv, link_send, link_recv, base_send, base_recv, home_send, home_recv,
@@ -179,8 +203,8 @@
     part = lambda index: pl.ds(pl.multiple_of(index * half, LANES), half)
     ours = part(mine)
     starts = [sum(node_count - LANES * i for i in range(j)) for j in range(blocks + 1)]
-    strip = (node_count - LANES) // 2
-    rest = (starts[blocks] - starts[2]) // 2
+    bounds = [0, LANES, starts[1] + LANES, starts[2], starts[blocks]]
+    heads, last = slice(0, node_count - LANES), slice(node_count - LANES, node_count)
 
     def copy(src, dst, send, recv, target):
         return pltpu.make_async_remote_copy(
@@ -273,10 +297,8 @@
     def piece(i):
         if i == 0:
             return pl.ds(0, LANES)
-        first, size = ((LANES, strip), (starts[1], strip), (starts[2], rest))[i - 1]
-        if i == 2:
-            size = (starts[2] - starts[1]) // 2
-        return pl.ds(pl.multiple_of(first + row_id * size, 8), size)
+        size = (bounds[i + 1] - bounds[i]) // 2
+        return pl.ds(pl.multiple_of(bounds[i] + row_id * size, ROWS), size)
 
     def up_copy(p, i):
         return copy(packed.at[1, piece(i)], landed.at[p, piece(i)], up_send.at[i], up_recv.at[p, i], {"tm": time_id + power(p)})
@@ -286,11 +308,9 @@
         return copy(tile, tile, pass_send.at[p, i], pass_recv.at[p, i], sibling)
 
     def link_copy(p, j):
-        rows = pl.ds(pl.multiple_of(mine * half + j * chunk, LANES), chunk)
-        return copy(
-            link_out.at[pl.ds(j * chunk, chunk)], links.at[p + 1, 0, rows, low], link_send.at[j], link_recv.at[p, j],
-            {"tm": time_id + power(p)},
-        )
+        src = link_out.at[pl.ds(j * chunk, chunk)]
+        dst = link_tile(p + 1, 0, j, "own") if j < 2 else link_tile(p + 1, 0, 0, "got")
+        return copy(src, dst, link_send.at[j], link_recv.at[p, j], {"tm": time_id + power(p)})
 
     def base_copy(p):
         return copy(base_out, base.at[p + 2, ours, low], base_send.at[0], base_recv.at[p], {"tm": time_id + power(p)})
@@ -328,7 +348,7 @@
 
             pivot_ref[1] = diag_ref[1]
             coupling_ref[1] = upper
-            packed[0] = jnp.zeros(packed.shape[1:], jnp.float32)
+            packed[...] = jnp.zeros(packed.shape, jnp.float32)
 
         work[...] = jnp.zeros(work.shape, jnp.float32)
         dr_copy(ph).wait_recv()
@@ -356,45 +376,64 @@
                 if shown:
                     final[below, rows, cols] = value + extra
 
-        def before(k):
-            for j in range(blocks):
-                @pl.when(k == j)
-                def _(j=j):
-                    if j in (1, 2):
-                        @pl.when(joined)
-                        def _():
-                            pass_copy(below, j + 1).wait_recv()
-                    if j == blocks // 2:
-                        @pl.when(leads)
-                        def _():
-                            df_copy(ph).wait_recv()
-                    if j == blocks - 1:
-                        @pl.when(later & solving)
-                        def _():
-                            link_copy(below, 1).wait_recv()
-                            start_link(ph, 0, 1)
-                    absorb(j, LANES * j, node_count if j else LANES)
+        def pivot_ready(j):
+            if j == 1:
+                absorb(j, LANES, 2 * LANES)
+                return
+            if j == 2:
+                @pl.when(joined)
+                def _():
+                    pass_copy(below, 3).wait_recv()
+            if j == blocks // 2:
+                @pl.when(leads)
+                def _():
+                    df_copy(ph).wait_recv()
+            if j == blocks - 1:
+                @pl.when(first)
+                def _():
+                    for i in (0, 1):
+                        end_link(0, 1, i)
+
+                @pl.when(later & solving)
+                def _():
+                    link_copy(below, 0).wait_recv()
+                    lr_copy(ph, 0, 0).start()
+            absorb(j, LANES * j, node_count if j else LANES)
+
+        def panel_ready(j):
+            if j == 0:
+                @pl.when(joined)
+                def _():
+                    pass_copy(below, 1).wait_recv()
+
+                absorb(0, LANES, node_count)
+            if j == 1:
+                @pl.when(joined)
+                def _():
+                    pass_copy(below, 2).wait_recv()
+
+                absorb(1, 2 * LANES, node_count)
 
         def middle(k):
-            @pl.when((k == 0) & joined)
-            def _():
-                up_copy(below, 1).wait_recv()
-                pass_copy(below, 1).start()
-
-            @pl.when(k == 1)
-            def _():
+            if k == 0:
                 @pl.when(joined)
                 def _():
-                    up_copy(below, 3).wait_recv()
-                    pass_copy(below, 3).start()
+                    up_copy(below, 1).wait_recv()
+                    pass_copy(below, 1).start()
+
+            if k == 1:
+                @pl.when(joined)
+                def _():
+                    for i in (2, 3):
+                        up_copy(below, i).wait_recv()
+                        pass_copy(below, i).start()
 
                 @pl.when(jnp.logical_not(leads))
                 def _():
                     dx_arrival(ph).wait_recv()
                     df_copy(ph).start()
 
-            @pl.when(k == 2)
-            def _():
+            if k == 2:
                 @pl.when(first)
                 def _():
                     for j in (0, 1):
@@ -402,8 +441,8 @@
 
                 @pl.when(later & solving)
                 def _():
-                    link_copy(below, 0).wait_recv()
-                    start_link(ph, 0, 0)
+                    link_copy(below, 1).wait_recv()
+                    start_link(ph, 0, 1)
 
                 @pl.when(later)
                 def _():
@@ -424,25 +463,48 @@
                         home_copy(ph, 0).start()
                         home_copy(ph, 1).start()
 
-            @pl.when((k == 3) & solving)
-            def _():
-                pass_link(ph, 0, 0)
-
-        def after(k):
-            @pl.when(k == 0)
-            def _():
-                @pl.when(joined)
-                def _():
-                    pass_copy(below, 1).wait_recv()
-
-                absorb(0, LANES, node_count)
-
-                @pl.when(joined)
-                def _():
-                    up_copy(below, 2).wait_recv()
-                    pass_copy(below, 2).start()
-
-        sweep_ref(work, before, middle, after)
+        def prepare():
+            own = links[ph, 1]
+            left = wide_left(own[:, heads])
+            beside = work[heads, last]
+            reached = mul(left, tall_right(work[heads, heads]))
+            part_solved[...] = reached
+            last_across[...] = beside
+            last_panel[...] = own[:, last] - mul(left, tall_right(beside))
+            for j in range(blocks):
+                rows = slice(LANES * j, LANES * (j + 1))
+                part_sum[starts[j] : starts[j + 1]] = mul_nt(left[LANES * j :], wide_right(reached[rows]))
+
+        def add_up(inverse):
+            ended = last_panel[...]
+            wide = wide_right(ended)
+            ahead = mul(wide_left(ended), tall_right(inverse))
+            last_solved[...] = ahead
+            left = wide_left(ahead)
+
+            def add(j, top, bottom):
+                lines = slice(starts[j] + top - LANES * j, starts[j] + bottom - LANES * j)
+                value = part_sum[lines] - mul_nt(left[top:bottom], wide[LANES * j : LANES * (j + 1)])
+                packed[1, lines] = packed[1, lines] + value
+
+            return add
+
+        def early(inverse):
+            @pl.when(sender)
+            def _():
+                add = add_up(inverse)
+                add(0, 0, LANES)
+                up_copy(ph, 0).start()
+                add(0, LANES, node_count)
+                add(1, LANES, 2 * LANES)
+                up_copy(ph, 1).start()
+                add(1, 2 * LANES, node_count)
+                up_copy(ph, 2).start()
+                for j in range(2, blocks):
+                    add(j, LANES * j, node_count)
+                up_copy(ph, 3).start()
+
+        sweep_ref(work, pivot_ready, panel_ready, middle, prepare, early)
 
         spot = pl.ds(pl.multiple_of(mine * half + col_id * (node_count // 4), LANES), node_count // 4)
         corner = work[spot, spot]
@@ -458,83 +520,69 @@
             log_out[ph] = jnp.broadcast_to(logs, log_out.shape[1:])
             home_copy(ph, 2).start()
 
-        @pl.when(solving)
-        def _():
+        def end_links():
+            @pl.when(first)
+            def _():
+                pass_link(0, 0, 0)
+
+            @pl.when(later)
+            def _():
+                link_copy(below, 2).wait_recv()
+                lf_copy(ph, 0, 0).start()
+
             pass_link(ph, 0, 1)
-
-            @pl.when(first)
-            def _():
-                for j in (0, 1):
-                    end_link(0, 1, j)
-
             for j in (0, 1):
                 end_link(ph, 0, j)
-            near, far = jnp.where(keeper, 0, 1), jnp.where(keeper, 1, 0)
-            inverse = tall_right(work[...])
-            left = wide_left(links[ph, near])
-            solved[...] = mul(left, inverse)
-
-            def panel(j):
-                return mul_nt(left[LANES * j :, :], wide_right(solved[LANES * j : LANES * (j + 1), :]))
-
-            def add_up(j, value):
-                lines = slice(starts[j], starts[j + 1])
-
-                @pl.when(first)
-                def _():
-                    packed[1, lines] = value
-
-                @pl.when(later)
-                def _():
-                    packed[1, lines] = packed[1, lines] + value
-
-            @pl.when(keeper)
-            def _():
+
+        @pl.when(keeper)
+        def _():
+            end_links()
+            left = wide_left(links[ph, 0])
+            solved[...] = mul(left, tall_right(work[...]))
+
+            @pl.when(later)
+            def _():
+                base_copy(below).wait_recv()
+                start_base(ph + 1)
+
+            for j in range(blocks):
+                rows = slice(LANES * j, LANES * (j + 1))
+                packed[0, starts[j] : starts[j + 1]] = mul_nt(left[LANES * j :], wide_right(solved[rows]))
+            links[ph + 1, 1] = mul_nt(wide_left(links[ph, 1]), wide_right(solved[...]))
+
+            @pl.when(time_id + 1 < times)
+            def _():
+                add = add_up(-work[last, last])
                 for j in range(blocks):
-                    packed[0, starts[j] : starts[j + 1]] = panel(j)
-
-                @pl.when(later)
-                def _():
-                    base_copy(below).wait_recv()
-                    start_base(ph + 1)
-
-                other = wide_left(links[ph, 1])
-                links[ph + 1, 1] = mul_nt(other, wide_right(solved[...]))
-
-                @pl.when(time_id + 1 < times)
-                def _():
-                    solved[...] = mul(other, inverse)
-                    for j in range(blocks):
-                        value = mul_nt(other[LANES * j :, :], wide_right(solved[LANES * j : LANES * (j + 1), :]))
-                        add_up(j, value)
-
-                @pl.when((ph == reach) & (time_id + power(reach) < times))
-                def _():
-                    for i in range(4):
-                        up_copy(reach, i).start()
-
-            @pl.when(sender)
-            def _():
-                for j in range(blocks):
-                    add_up(j, panel(j))
-                    if j == 0:
-                        up_copy(ph, 0).start()
-                        up_copy(ph, 1).start()
-                    if j == 1:
-                        up_copy(ph, 2).start()
-                up_copy(ph, 3).start()
-                other = wide_left(links[ph, 0, ours])
-                link_out[...] = mul_nt(other, wide_right(solved[0:half, :]))
-                for j in (0, 1):
-                    link_copy(ph, j).start()
-
-                @pl.when(later)
-                def _():
-                    base_copy(below).wait_recv()
-
-                reached = mul(wide_left(links[ph, 0, low]), inverse)
-                base_out[...] = base[ph + 1, ours, low] + mul_nt(other, wide_right(reached))
-                base_copy(ph).start()
+                    add(j, LANES * j, node_count)
+
+            @pl.when((ph == reach) & (time_id + power(reach) < times))
+            def _():
+                for i in range(4):
+                    up_copy(reach, i).start()
+
+        @pl.when(sender)
+        def _():
+            end_links()
+            ahead = last_solved[...]
+            solved[:, heads] = part_solved[...] + mul_nt(wide_left(ahead), wide_right(last_across[...]))
+            solved[:, last] = -ahead
+            other = wide_left(links[ph, 0, ours])
+            wide = wide_right(solved[...])
+            link_out[chunk:half] = mul_nt(other[chunk:], wide[:half])
+            link_copy(ph, 1).start()
+            link_out[0:chunk] = mul_nt(other[:chunk], wide[:half])
+            link_copy(ph, 0).start()
+            link_out[half:] = mul_nt(other[:chunk], wide[half:])
+            link_copy(ph, 2).start()
+
+            @pl.when(later)
+            def _():
+                base_copy(below).wait_recv()
+
+            reached = mul(wide_left(links[ph, 0, low]), tall_right(work[...]))
+            base_out[...] = base[ph + 1, ours, low] + mul_nt(other, wide_right(reached))
+            base_copy(ph).start()
 
         return carry
 
@@ -550,7 +598,6 @@
 
     def drain(ph, carry):
         below = jnp.maximum(ph - 1, 0)
-        dr = (ph > 0) | (ph == 0)
         dr_copy(ph).wait_send()
 
         @pl.when(leads)
@@ -563,7 +610,10 @@
 
         def link_sends(slot):
             for j in (0, 1):
-                lx_copy(ph, slot, j).wait_send()
+                @pl.when((ph == 0) | (j == 1))
+                def _(j=j):
+                    lx_copy(ph, slot, j).wait_send()
+
                 lr_copy(ph, slot, j).wait_send()
                 lf_copy(ph, slot, j).wait_send()
 
@@ -596,7 +646,7 @@
 
     @pl.when(depth < reach)
     def _():
-        for j in (0, 1):
+        for j in range(3):
             link_copy(depth, j).wait_send()
         base_copy(depth).wait_send()
 
@@ -605,7 +655,7 @@
     half = precision_diag.shape[1]
     node_count = 2 * half
     blocks = node_count // LANES
-    lines = LANES * LANES // LANES * blocks * (blocks + 1) // 2
+    lines = LANES * blocks * (blocks + 1) // 2
     vmem = pl.BlockSpec(memory_space=pltpu.VMEM)
     dma = pltpu.SemaphoreType.DMA
     real = lambda *shape: pltpu.VMEM(shape, jnp.float32)
@@ -625,15 +675,20 @@
             real(2, lines, LANES),
             real(LEVELS, lines, LANES),
             real(LEVELS, node_count, half),
-            real(half, half),
+            real(half + half // 2, half),
             real(half, half),
             real(2, half, half),
             real(phases, ROWS, node_count // 4),
             real(ROWS, node_count // 4),
+            real(lines, LANES),
+            real(node_count, node_count - LANES),
+            real(node_count, LANES),
+            real(node_count - LANES, LANES),
+            real(node_count, LANES),
             dma((phases,)), dma((phases,)), dma((phases,)), dma((phases,)), dma((phases,)), dma((phases,)),
             dma(pair), dma(pair), dma(pair), dma(pair), dma(pair), dma(pair),
             dma((4,)), dma((LEVELS, 4)), dma((LEVELS, 4)), dma((LEVELS, 4)),
-            dma((2,)), dma((LEVELS, 2)), dma((1,)), dma((LEVELS,)), dma((phases, 3)), dma((3,)),
+            dma((3,)), dma((LEVELS, 3)), dma((1,)), dma((LEVELS,)), dma((phases, 3)), dma((3,)),
         ],
         compiler_params=pltpu.CompilerParams(collective_id=0, has_side_effects=True),
     )(precision_diag, precision_link)

time: 141 us -> 125 us (0.89)
  Pallas kernels: 137 us -> 121 us
    pallas_call x1, Pallas kernels: 137 us -> 121 us  [shards(): pl.pallas_call(cyclic_kernel, out_shape=(stack, stack, jax.ShapeDtypeStru...]
where the time goes in v2:
time: 125 us
  Pallas kernels  121 us (97%)
  local copies, waits for them, and re-layouts  3.29 us (3%)
    pallas_call x1, Pallas kernels, shards(): pl.pallas_call(cyclic_kernel, out_shape=(stack, stack, jax.ShapeDtypeStru...  121 us
    unnamed x7, local copies, waits for them, and re-layouts  3.29 us

profile of v2, /device:TPU:0, one launch (start us, length us, event | category | flops | bytes accessed | tf_op | source)
XLA Modules:
  0.0 124.7 jit_solution(1646871097647142358)
XLA Ops:
  0.6 120.7 %shard_map.49 = (f32[2,256,256]{2,1,0:T(8,128)}, f32[2,256,256]{2,1,0:T(8,128)}, f32[2,128]{1,0:T(2,128)}) custom-call(f32[2,256,256]{2,1,0:T(8,128)} %diag_ref.1, f32[2,256,256]{2,1,0:T(8,128)} %link_ref.1), custom_call_target="tpu_custom_call" | custom-call | tf_op jit(solution)/shard_map/pallas_call | solution.py:665
  121.4 0.0 copy-start
  121.4 1.9 %copy.8 = f32[2,256,256]{2,1,0:T(8,128)} copy(f32[2,256,256]{2,1,0:T(8,128)} %get-tuple-element.6) | data formatting | bytes 1048576
  123.3 0.0 copy-done
  123.3 0.0 copy-start.1
  123.3 0.8 copy.9
  124.1 0.0 copy-done.1
  124.1 0.6 copy.10
Async XLA Ops:
  121.4 1.9 %copy-start = (f32[2,256,256]{2,1,0:T(8,128)S(1)}, f32[2,256,256]{2,1,0:T(8,128)}, u32[]{:S(2)}) copy-start(f32[2,256,256]{2,1,0:T(8,128)} %get-tuple-element.7) | copy-start | bytes 1572868
  123.3 0.8 copy-start.1
